TPU v7x, 32 devices: a whole 2x2x4 slice. The times are simulated.
32 devices in a mesh: head: 4 (over z), batch: 8 (over y, x, core).
Axes of the slice: x: 2, y: 2, z: 4, core: 2. Of those that a mesh axis runs over, the one named last changes fastest.
Arguments:
- window_ids: int32 [32, 22], replicated, may hold values from 0 to 64127
- pool_ids: int32 [32, 64, 3], replicated, may hold values from 0 to 64127
- guess_index: int32 [32, 7], replicated, may hold values from 0 to 63
- lengths: int32 [32], P('batch'), may hold values from 16 to 2048, as said below
- embed_table: bfloat16 [64128, 8192], P('batch', 'head'), may hold values from -6 to 6
- w_query: bfloat16 [8192, 8192], P('batch', 'head'), may hold values from -0.0625 to 0.0625
- w_key: bfloat16 [8192, 1024], P('batch', 'head'), may hold values from -0.0625 to 0.0625
- w_value: bfloat16 [8192, 1024], P('batch', 'head'), may hold values from -0.0625 to 0.0625
- k_cache: bfloat16 [8, 32, 2048, 128], P(None, None, ('head', 'batch')), may hold values from -300 to 300
- v_cache: bfloat16 [8, 32, 2048, 128], P(None, None, ('head', 'batch')), may hold values from -12 to 12
Outputs:
- attended: bfloat16 [1376, 8192], P('batch', 'head')
- k_decode: bfloat16 [8, 32, 2048, 128], P('head', 'batch')
- v_decode: bfloat16 [8, 32, 2048, 128], P('head', 'batch')
Inputs may be any that keep to these rules, and one draw needn't show every extreme that they name: `lengths`: in every draw one sequence has exactly 2048 cached tokens.
All inputs are finite; a program needn't handle non-finite values.
Results may differ from a plain program's by a relative error of at most 0.0055.
The roundings to bfloat16 on the way count: a program that leaves them out, or rounds other values in their place, can miss the bound.
Values may be sent and summed in bfloat16 or wider, within the bound.
No kernel may reach another device: no remote copies, remote signals or barrier semaphores. Data moves between devices by JAX's collectives and lax.ppermute only.
A program may use at most 192 MiB of HBM per device.

v0:
```python
import jax
import jax.numpy as jnp
import numpy as np
from jax import lax
from jax.sharding import PartitionSpec as P

W = 7
NG = 4
G = 7
ROPE_BASE = 500000.0
NORM_EPS = 1e-05


def layout_tables():
    levels = NG - 1
    level_of = np.repeat(np.arange(levels), W)
    column_of = np.tile(np.arange(W), levels)
    window_mask = (level_of[None, :] == 0) & (column_of[None, :] <= column_of[:, None]) | (
        column_of[None, :] == column_of[:, None]
    ) & (level_of[None, :] <= level_of[:, None])
    guess_of = np.repeat(np.arange(G), levels)
    slot_of = np.tile(np.arange(levels), G)
    guess_mask = (guess_of[None, :] == guess_of[:, None]) & (slot_of[None, :] <= slot_of[:, None])
    window_rows = levels * W
    total_rows = 1 + window_rows + G * levels
    allowed = np.zeros((total_rows, total_rows), np.bool_)
    allowed[:, 0] = True
    allowed[1 : 1 + window_rows, 1 : 1 + window_rows] = window_mask
    allowed[1 + window_rows :, 1 + window_rows :] = guess_mask
    offsets = np.concatenate(
        [
            np.zeros(1, np.int32),
            (1 + level_of + column_of).astype(np.int32),
            (1 + slot_of).astype(np.int32),
        ]
    )
    return (offsets, allowed)


def gather_ids(window_ids, pool_ids, guess_index):
    wanted = jnp.broadcast_to(
        guess_index[:, :, None], (guess_index.shape[0], guess_index.shape[1], pool_ids.shape[2])
    )
    picked = jnp.take_along_axis(pool_ids, wanted, axis=1)
    return jnp.concatenate([window_ids, picked.reshape(picked.shape[0], -1)], axis=1)


def rotate(vectors, positions):
    head_dim = vectors.shape[-1]
    half_dim = head_dim // 2
    ladder = jnp.arange(half_dim).astype(jnp.float32)
    frequencies = jnp.power(ROPE_BASE, ladder * (-2.0 / head_dim))
    angles = positions.astype(jnp.float32)[..., None] * frequencies
    cosine = jnp.cos(angles)[..., None, :]
    sines = jnp.sin(angles)[..., None, :]
    front_half = vectors[..., :half_dim]
    second = vectors[..., half_dim:]
    return jnp.concatenate(
        [front_half * cosine - second * sines, second * cosine + front_half * sines], axis=-1
    )


def per_device(
    window_ids,
    pool_ids,
    guess_index,
    lengths,
    embed_table,
    w_query,
    w_key,
    w_value,
    k_cache,
    v_cache,
):
    offsets, allowed = layout_tables()
    total_rows = offsets.shape[0]
    n_head = lax.axis_size("head")
    n_batch = lax.axis_size("batch")
    kv_total, seq_total, slab, head_dim = k_cache.shape
    kv_dev = kv_total // n_head
    seq_dev = seq_total // n_batch
    token_ids = gather_ids(window_ids, pool_ids, guess_index).reshape(-1)
    vocab_rows = embed_table.shape[0]
    local_ids = token_ids - lax.axis_index("batch") * vocab_rows
    inside = (local_ids >= 0) & (local_ids < vocab_rows)
    found_rows = jnp.take(embed_table, jnp.clip(local_ids, 0, vocab_rows - 1), axis=0)
    partial_rows = jnp.where(inside[:, None], found_rows.astype(jnp.float32), 0.0)
    embedded = lax.psum_scatter(
        partial_rows.astype(jnp.bfloat16), "batch", scatter_dimension=0, tiled=True
    )
    embedded = lax.all_gather(embedded, "head", axis=1, tiled=True)
    widened = embedded.astype(jnp.float32)
    normed = (
        widened * lax.rsqrt(jnp.mean(widened * widened, axis=-1, keepdims=True) + NORM_EPS)
    ).astype(jnp.bfloat16)
    pieces = (
        lax.all_gather(w_query, "batch", axis=0, tiled=True),
        lax.all_gather(w_key, "batch", axis=0, tiled=True),
        lax.all_gather(w_value, "batch", axis=0, tiled=True),
    )
    query_raw, key_raw, value_raw = tuple(
        (jnp.dot(normed, piece_part, preferred_element_type=jnp.float32) for piece_part in pieces)
    )
    q_heads = w_query.shape[1] // head_dim
    per_group = q_heads // kv_dev
    positions = lengths[:, None] + jnp.asarray(offsets).astype(jnp.int32)[None, :]
    queries = rotate(query_raw.reshape(seq_dev, total_rows, q_heads, head_dim), positions).astype(
        jnp.bfloat16
    )
    keys_new = rotate(key_raw.reshape(seq_dev, total_rows, kv_dev, head_dim), positions).astype(
        jnp.bfloat16
    )
    values_new = value_raw.astype(jnp.bfloat16).reshape(seq_dev, total_rows, kv_dev, head_dim)

    def arrange(kv_block):
        shaped = kv_block.reshape(n_head, kv_dev, n_batch, seq_dev, slab, head_dim)
        return jnp.swapaxes(shaped, 1, 2)

    context = slab * n_head * n_batch
    flat_k = arrange(k_cache).reshape(n_head * n_batch, kv_dev, seq_dev, slab, head_dim)
    flat_v = arrange(v_cache).reshape(n_head * n_batch, kv_dev, seq_dev, slab, head_dim)
    k_here, v_here = (
        lax.all_to_all(flat_k, ("head", "batch"), split_axis=0, concat_axis=3, tiled=True),
        lax.all_to_all(flat_v, ("head", "batch"), split_axis=0, concat_axis=3, tiled=True),
    )
    k_here = k_here.reshape(kv_dev, seq_dev, context, head_dim)
    v_here = v_here.reshape(kv_dev, seq_dev, context, head_dim)
    q_five = queries.reshape(seq_dev, total_rows, kv_dev, per_group, head_dim)
    score_scale = head_dim ** (-0.5)
    old_scores = (
        jnp.einsum("stkgd,kscd->skgtc", q_five, k_here, preferred_element_type=jnp.float32)
        * score_scale
    )
    new_scores = (
        jnp.einsum("stkgd,sukd->skgtu", q_five, keys_new, preferred_element_type=jnp.float32)
        * score_scale
    )
    visible = jnp.arange(context)[None, :] < lengths[:, None]
    old_scores = jnp.where(visible[:, None, None, None, :], old_scores, -1e30)
    new_scores = jnp.where(jnp.asarray(allowed), new_scores, -1e30)
    row_peak = jnp.maximum(
        jnp.max(old_scores, axis=-1, keepdims=True), jnp.max(new_scores, axis=-1, keepdims=True)
    )
    old_powers = jnp.exp(old_scores - row_peak)
    new_powers = jnp.exp(new_scores - row_peak)
    denominator = jnp.sum(old_powers, axis=-1, keepdims=True) + jnp.sum(
        new_powers, axis=-1, keepdims=True
    )
    old_weights = (old_powers / denominator).astype(jnp.bfloat16)
    new_weights = (new_powers / denominator).astype(jnp.bfloat16)
    blended = jnp.einsum(
        "skgtc,kscd->stkgd", old_weights, v_here, preferred_element_type=jnp.float32
    )
    blended = blended + jnp.einsum(
        "skgtu,sukd->stkgd", new_weights, values_new, preferred_element_type=jnp.float32
    )
    attended = blended.astype(jnp.bfloat16).reshape(seq_dev * total_rows, q_heads * head_dim)
    return (attended, k_here, v_here)


def solution(mesh):
    placed = (
        P(),
        P(),
        P(),
        P("batch"),
        P("batch", "head"),
        P("batch", "head"),
        P("batch", "head"),
        P("batch", "head"),
        P(None, None, ("head", "batch"), None),
        P(None, None, ("head", "batch"), None),
    )
    return jax.shard_map(
        per_device,
        mesh=mesh,
        in_specs=placed,
        out_specs=(
            P("batch", "head"),
            P("head", "batch", None, None),
            P("head", "batch", None, None),
        ),
        check_vma=False,
    )
```

profile of v0, /device:TPU:0, one launch (start us, length us, event | category | flops | bytes accessed | tf_op | source)
XLA Modules:
  0.0 621.6 jit_solution(6536742778525920510)
XLA Ops:
  10.0 9.1 %gather_fusion.1 = s32[672]{0:T(1024)S(1)} fusion(s32[32,64,3]{1,0,2:T(8,128)S(1)} %copy-done, s32[672]{0:T(1024)S(1)} %reshape.206), kind=kCustom, calls=%fused_computation.1 | custom fusion | bytes 13440 | tf_op jit(solution)/shard_map/jit(take_along_axis)/gather | solution.py:44
  20.2 56.0 %gather_fusion = bf16[1376,2048]{1,0:T(8,128)(2,1)} fusion(bf16[8016,2048]{1,0:T(8,128)(2,1)} %param.16, s32[2048]{0:T(1024)S(1)} %pad_clamp_fusion), kind=kCustom, calls=%fused_computation | custom fusion | bytes 11277696 | tf_op jit(solution)/shard_map/jit(_take)/gather | solution.py:86
  76.2 7.0 %select_convert_fusion = bf16[1376,2048]{1,0:T(8,128)(2,1)} fusion(bf16[1376,2048]{1,0:T(8,128)(2,1)} %gather_fusion, pred[1376]{0:T(1024)(128)(4,1)S(1)} %compare_and_fusion.1, pred[1376]{0:T(1024)(128)(4,1)S(1)} %and.29), kind=kLoop, calls=%fused_computation.8 | loop fusion | flops 11272192 | bytes 11274944 | tf_op jit(solution)/shard_map/convert_element_type | solution.py:89
  83.2 60.9 %fusion = bf16[176,2048]{1,0:T(8,128)(2,1)S(1)} fusion(bf16[1376,2048]{1,0:T(8,128)(2,1)} %select_convert_fusion), kind=kCustom, calls=%all-reduce-scatter | all-reduce-scatter fusion | flops 2883585 | bytes 6357504
  146.7 1.5 concatenate.25
  151.3 5.6 copy.121
  156.9 10.1 %all-to-all-start = ((bf16[32,2,4,64,128]{4,3,1,2,0:T(8,128)(2,1)}), bf16[32,2,4,64,128]{4,3,1,2,0:T(8,128)(2,1)}, u32[]{:S(2)}, u32[]{:S(2)}) async-start(bf16[32,2,4,64,128]{4,3,1,2,0:T(8,128)(2,1)} %bitcast.80), calls=%async_computation | async-start | bytes 8388608 | tf_op jit(solution)/shard_map/all_to_all | solution.py:123
  167.0 5.6 copy.130
  172.6 130.5 %all-to-all-done = bf16[32,2,4,64,128]{4,3,1,2,0:T(8,128)(2,1)} async-done(((bf16[32,2,4,64,128]{4,3,1,2,0:T(8,128)(2,1)}), bf16[32,2,4,64,128]{4,3,1,2,0:T(8,128)(2,1)}, u32[]{:S(2)}, u32[]{:S(2)}) %all-to-all-start) | async-done | bytes 4194336 | tf_op jit(solution)/shard_map/all_to_all | solution.py:123
  303.1 3.9 all-to-all-start.1
  307.6 2.6 fusion.4
  310.2 28.7 %all-gather.9.cloned.1.call-done = bf16[8192,256]{1,0:T(8,128)(2,1)} async-done(((bf16[1024,256]{1,0:T(8,128)(2,1)}), bf16[8192,256]{1,0:T(8,128)(2,1)}) %all-gather.9.cloned.1.call-update) | async-done | bytes 4194320 | tf_op jit(solution)/shard_map/all_gather | solution.py:98
  338.9 4.0 fusion.25
  343.1 57.4 %all-gather.11.cloned.1.call-done = bf16[8192,256]{1,0:T(8,128)(2,1)} async-done(((bf16[1024,256]{1,0:T(8,128)(2,1)}), bf16[8192,256]{1,0:T(8,128)(2,1)}) %all-gather.11.cloned.1.call-update) | async-done | bytes 4194320 | tf_op jit(solution)/shard_map/all_gather | solution.py:99
  400.5 3.1 convolution_convert_fusion
  404.0 6.0 copy.122
  410.0 4.2 copy.131
  415.0 2.7 copy.135
  418.2 2.3 copy.136
  420.5 141.8 %all-gather.7.cloned.1.call-done = bf16[8192,2048]{1,0:T(8,128)(2,1)} async-done(((bf16[1024,2048]{1,0:T(8,128)(2,1)}), bf16[8192,2048]{1,0:T(8,128)(2,1)}) %all-gather.7.cloned.1.call-update) | async-done | bytes 33554448 | tf_op jit(solution)/shard_map/all_gather | solution.py:97
  562.3 13.7 %fusion.27 = f32[172,2048]{1,0:T(8,128)S(1)} fusion(bf16[8192,2048]{1,0:T(8,128)(2,1)} %all-gather.7.cloned.1.call-done, bf16[172,8192]{1,0:T(8,128)(2,1)S(1)} %copy-done.5, f32[172]{0:T(256)S(1)} %add_rsqrt_fusion), kind=kOutput, calls=%fused_computation.63 | convolution fusion | flops 5775589376 | bytes 37782192 | tf_op jit(solution)/shard_map/dot_general | solution.py:102
  578.5 9.3 %bitcast_reduce_fusion = (f32[4,2,8,43]{2,3,1,0:T(8,128)S(1)}, f32[4,2,43,8,2048]{4,3,2,1,0:T(8,128)}) fusion(pred[4,2048]{1,0:T(4,128)(4,1)S(1)} %iota_compare_fusion, bf16[2,4,2048,128,1]{3,2,4,0,1:T(8,128)(2,1)S(1)} %bitcast.76, bf16[4,43,2,8,128]{4,3,2,1,0:T(8,128)(2,1)S(1)} %pad_maximum_fusion), kind=kOutput, calls=%fused_computation.3 | convolution fusion | flops 1459746048 | bytes 27462400 | tf_op jit(solution)/shard_map/stkgd,kscd->skgtc/dot_general | solution.py:131
  589.6 10.9 %fusion.2 = f32[4,2,8,43]{2,3,1,0:T(8,128)S(1)} fusion(f32[4,2,43,8,2048]{4,3,2,1,0:T(8,128)} %get-tuple-element.27, f32[4,2,8,43]{2,3,1,0:T(8,128)S(1)} %copy.127, pred[4,2048]{1,0:T(4,128)(4,1)S(1)} %iota_compare_fusion), kind=kLoop, calls=%fused_computation.7 | loop fusion | flops 22541632 | bytes 22574592 | tf_op jit(solution)/shard_map/reduce_sum | solution.py:146
  601.7 11.5 %fusion.7 = f32[4,43,2,8,128]{4,3,1,2,0:T(8,128)S(1)} fusion(bf16[2,4,2048,128,1]{3,2,4,0,1:T(8,128)(2,1)} %bitcast.78, f32[4,2,43,8,2048]{4,3,2,1,0:T(8,128)} %get-tuple-element.27, f32[4,2,8,43]{2,3,1,0:T(8,128)S(1)} %copy.129, f32[4,2,8,43]{2,3,1,0:T(8,128)S(1)} %copy.127, pred[4,2048]{1,0:T(4,128)(4,1)S(1)} %iota_compare_fusion), kind=kOutput, calls=%fused_computation.19 | convolution fusion | flops 1471021056 | bytes 28177920 | tf_op jit(solution)/shard_map/skgtc,kscd->stkgd/dot_general | solution.py:151
  (82 shorter events, 18.3 us)
Async XLA Ops:
  7.2 2.8 copy-start
  7.2 300.4 %all-gather.5.cloned.1.call-start = ((), (), s32[]{:S(2)}) async-start(), calls=%async_computation.2 | async-start | bytes 3604480 | tf_op jit(solution)/shard_map/all_gather | solution.py:91
  10.0 9.6 %copy-start.6 = (s32[32,22]{0,1:T(8,128)S(1)}, s32[32,22]{0,1:T(8,128)}, u32[]{:S(2)}) copy-start(s32[32,22]{0,1:T(8,128)} %param.12) | copy-start | bytes 8452
  83.2 62.3 %copy-start.9 = (u32[32]{0:T(128)S(1)}, u32[32]{0:T(128)}, u32[]{:S(2)}) copy-start(u32[32]{0:T(128)} %constant.86) | copy-start | bytes 388
  144.1 2.6 collective-permute-start
  149.2 189.7 %all-gather.9.cloned.1.call-start = ((), (), s32[]{:S(2)}) async-start(), calls=%async_computation.4 | async-start | bytes 4718592 | tf_op jit(solution)/shard_map/all_gather | solution.py:98
  150.0 250.5 %all-gather.11.cloned.1.call-start = ((), (), s32[]{:S(2)}) async-start(), calls=%async_computation.5 | async-start | bytes 4718592 | tf_op jit(solution)/shard_map/all_gather | solution.py:99
  150.7 411.6 %all-gather.7.cloned.1.call-start = ((), (), s32[]{:S(2)}) async-start(), calls=%async_computation.3 | async-start | bytes 37748736 | tf_op jit(solution)/shard_map/all_gather | solution.py:97
  156.9 146.2 %all-to-all-start = ((bf16[32,2,4,64,128]{4,3,1,2,0:T(8,128)(2,1)}), bf16[32,2,4,64,128]{4,3,1,2,0:T(8,128)(2,1)}, u32[]{:S(2)}, u32[]{:S(2)}) async-start(bf16[32,2,4,64,128]{4,3,1,2,0:T(8,128)(2,1)} %bitcast.80), calls=%async_computation | async-start | bytes 8388608 | tf_op jit(solution)/shard_map/all_to_all | solution.py:123
  303.1 3.9 copy-start.8
  303.1 3.9 copy-start.10
  303.1 106.9 %all-to-all-start.1 = ((bf16[32,2,4,64,128]{4,3,1,2,0:T(8,128)(2,1)}), bf16[32,2,4,64,128]{4,3,1,2,0:T(8,128)(2,1)}, u32[]{:S(2)}, u32[]{:S(2)}) async-start(bf16[32,2,4,64,128]{4,3,1,2,0:T(8,128)(2,1)} %bitcast.79), calls=%async_computation.1 | async-start | bytes 8388608 | tf_op jit(solution)/shard_map/all_to_all | solution.py:124
  310.2 90.3 %copy-start.5 = (bf16[172,8192]{1,0:T(8,128)(2,1)S(1)}, bf16[172,8192]{1,0:T(8,128)(2,1)}, u32[]{:S(2)}) copy-start(bf16[172,8192]{1,0:T(8,128)(2,1)} %all-gather.5.cloned.1.call-done) | copy-start | bytes 8454148
  410.0 5.0 copy-start.2
  414.2 4.0 copy-start.4
  576.3 2.2 copy-start.3
  578.5 9.4 %copy-start.7 = (pred[43,43]{0,1:T(8,128)(4,1)S(1)}, pred[43,43]{0,1:T(8,128)(4,1)}, u32[]{:S(2)}) copy-start(pred[43,43]{0,1:T(8,128)(4,1)} %constant.63.clone) | copy-start | bytes 5551
  601.7 13.4 %copy-start.1 = (s32[32,64,3]{1,0,2:T(8,128)S(1)}, s32[32,64,3]{1,0,2:T(8,128)}, u32[]{:S(2)}) copy-start(s32[32,64,3]{1,0,2:T(8,128)} %param.13) | copy-start | bytes 73732
Sparse Core Ops, SparseCore 0:
  149.4 121.8 all-gather.4
  273.2 65.6 all-gather.8
  340.8 59.6 all-gather.10
  402.2 160.0 all-gather.6
where the time goes:
time: 623 us; the launch traced here: 622 us
  waiting for transfers between devices  360 us (58%)
  local copies, waits for them, and re-layouts  102 us (16%)
  blocking collectives  60.9 us (10%)
  matrix products  43.3 us (7%)
  other arithmetic  24.8 us (4%)
  starting transfers between devices  15.4 us (2%)
  between operations  14.8 us (2%)
    all_gather x1, waiting for transfers between devices, per_device(): lax.all_gather(w_query, 'batch', axis=0, tiled=True)  142 us
    all_to_all x1, waiting for transfers between devices, per_device(): lax.all_to_all(flat_k, ('head', 'batch'), split_axis=0, concat_axis=3, ti...  130 us
    unnamed x1, blocking collectives  60.9 us
    all_gather x1, waiting for transfers between devices, per_device(): lax.all_gather(w_value, 'batch', axis=0, tiled=True)  57.4 us
    gather x1, local copies, waits for them, and re-layouts, per_device(): jnp.take(embed_table, jnp.clip(local_ids, 0, vocab_rows - 1), axis=0)  56 us
    all_gather x1, waiting for transfers between devices, per_device(): lax.all_gather(w_key, 'batch', axis=0, tiled=True)  28.7 us
    dot_general x3, matrix products, per_device(): jnp.dot(normed, piece_part, preferred_element_type=jnp.float32)  20.9 us
  transfers between devices with their start and end apart: 7, of which 4 were waited for; matrix products, arithmetic and copies ran while one was open for 6% of the time, Pallas kernels for 0%

commit v1 on v0

--- a/solution.py
+++ b/solution.py
@@ -9,6 +9,13 @@
 G = 7
 ROPE_BASE = 500000.0
 NORM_EPS = 1e-05
+
+
+def trade_parts(x, axis, split, join):
+    count = lax.axis_size(axis)
+    pieces = jnp.stack(jnp.split(x, count, axis=split), axis=0)
+    pieces = lax.all_to_all(pieces, axis, split_axis=0, concat_axis=0)
+    return jnp.concatenate(pieces, axis=join)
 
 
 def layout_tables():
@@ -120,7 +127,7 @@
     flat_k = arrange(k_cache).reshape(n_head * n_batch, kv_dev, seq_dev, slab, head_dim)
     flat_v = arrange(v_cache).reshape(n_head * n_batch, kv_dev, seq_dev, slab, head_dim)
     k_here, v_here = (
-        lax.all_to_all(flat_k, ("head", "batch"), split_axis=0, concat_axis=3, tiled=True),
+        trade_parts(flat_k, ("head", "batch"), 0, 3),
         lax.all_to_all(flat_v, ("head", "batch"), split_axis=0, concat_axis=3, tiled=True),
     )
     k_here = k_here.reshape(kv_dev, seq_dev, context, head_dim)

time: 623 us -> 602 us (0.966)
  waiting for transfers between devices: 360 us -> 325 us
  local copies, waits for them, and re-layouts: 102 us -> 118 us
    all_gather x1, waiting for transfers between devices: 28.7 us -> 0.02 us  [per_device(): lax.all_gather(w_key, 'batch', axis=0, tiled=True)]
    all_to_all x1, waiting for transfers between devices: 0.01 us -> 20.3 us  [per_device(): lax.all_to_all(flat_v, ('head', 'batch'), split_axis=0, concat_axis=3, ti...]
    unnamed x32 -> x65, local copies, waits for them, and re-layouts: 11.6 us -> 31.6 us
    all_to_all x1, waiting for transfers between devices: 130 us -> 112 us  [trade_parts(): pieces = lax.all_to_all(pieces, axis, split_axis=0, concat_axis=0)]
    all_gather x1, waiting for transfers between devices: 142 us -> 132 us  [per_device(): lax.all_gather(w_query, 'batch', axis=0, tiled=True)]
  transfers between devices with their start and end apart: 7 -> 7, of which waited for: 4 -> 4; matrix products, arithmetic and copies ran while one was open for 6% -> 9% of each run, Pallas kernels for 0% -> 0%
where the time goes in v1:
time: 602 us; the launch traced here: 601 us
  waiting for transfers between devices  325 us (54%)
  local copies, waits for them, and re-layouts  118 us (20%)
  blocking collectives  60.9 us (10%)
  matrix products  44.4 us (7%)
  other arithmetic  22.8 us (4%)
  starting transfers between devices  15.4 us (3%)
  between operations  14.8 us (2%)
    all_gather x1, waiting for transfers between devices, per_device(): lax.all_gather(w_query, 'batch', axis=0, tiled=True)  132 us
    all_to_all x1, waiting for transfers between devices, trade_parts(): pieces = lax.all_to_all(pieces, axis, split_axis=0, concat_axis=0)  112 us
    unnamed x1, blocking collectives  60.9 us
    all_gather x1, waiting for transfers between devices, per_device(): lax.all_gather(w_value, 'batch', axis=0, tiled=True)  58 us
    gather x1, local copies, waits for them, and re-layouts, per_device(): jnp.take(embed_table, jnp.clip(local_ids, 0, vocab_rows - 1), axis=0)  56 us
    unnamed x65, local copies, waits for them, and re-layouts  31.6 us
    dot_general x3, matrix products, per_device(): jnp.dot(normed, piece_part, preferred_element_type=jnp.float32)  21.2 us
    all_to_all x1, waiting for transfers between devices, per_device(): lax.all_to_all(flat_v, ('head', 'batch'), split_axis=0, concat_axis=3, ti...  20.3 us
  transfers between devices with their start and end apart: 7, of which 4 were waited for; matrix products, arithmetic and copies ran while one was open for 9% of the time, Pallas kernels for 0%

profile of v1, /device:TPU:0, one launch (start us, length us, event | category | flops | bytes accessed | tf_op | source)
XLA Modules:
  0.0 601.0 jit_solution(14945582079892933239)
XLA Ops:
  10.0 9.1 %gather_fusion.1 = s32[672]{0:T(1024)S(1)} fusion(s32[32,64,3]{1,0,2:T(8,128)S(1)} %copy-done, s32[672]{0:T(1024)S(1)} %reshape.205), kind=kCustom, calls=%fused_computation.1 | custom fusion | bytes 13440 | tf_op jit(solution)/shard_map/jit(take_along_axis)/gather | solution.py:51
  20.2 56.0 %gather_fusion = bf16[1376,2048]{1,0:T(8,128)(2,1)} fusion(bf16[8016,2048]{1,0:T(8,128)(2,1)} %param.16, s32[2048]{0:T(1024)S(1)} %pad_clamp_fusion), kind=kCustom, calls=%fused_computation | custom fusion | bytes 11277696 | tf_op jit(solution)/shard_map/jit(_take)/gather | solution.py:93
  76.2 7.0 %select_convert_fusion = bf16[1376,2048]{1,0:T(8,128)(2,1)} fusion(bf16[1376,2048]{1,0:T(8,128)(2,1)} %gather_fusion, pred[1376]{0:T(1024)(128)(4,1)S(1)} %compare_and_fusion.1, pred[1376]{0:T(1024)(128)(4,1)S(1)} %and.29), kind=kLoop, calls=%fused_computation.9 | loop fusion | flops 11272192 | bytes 11274944 | tf_op jit(solution)/shard_map/convert_element_type | solution.py:96
  83.2 60.9 %fusion = bf16[176,2048]{1,0:T(8,128)(2,1)S(1)} fusion(bf16[1376,2048]{1,0:T(8,128)(2,1)} %select_convert_fusion), kind=kCustom, calls=%all-reduce-scatter | all-reduce-scatter fusion | flops 2883585 | bytes 6357504
  146.7 1.5 concatenate.24
  151.3 3.1 copy.134
  175.7 10.1 %all-to-all-start = ((bf16[32,1,2,4,64,128]{5,4,2,3,1,0:T(8,128)(2,1)}), bf16[32,1,2,4,64,128]{5,4,2,3,1,0:T(8,128)(2,1)}, u32[]{:S(2)}, u32[]{:S(2)}) async-start(bf16[32,1,2,4,64,128]{5,4,2,3,1,0:T(8,128)(2,1)} %fusion.10), calls=%async_computation | async-start | bytes 8388608 | tf_op jit(solution)/shard_map/all_to_all | solution.py:17
  185.8 5.6 copy.149
  191.4 112.3 %all-to-all-done = bf16[32,1,2,4,64,128]{5,4,2,3,1,0:T(8,128)(2,1)} async-done(((bf16[32,1,2,4,64,128]{5,4,2,3,1,0:T(8,128)(2,1)}), bf16[32,1,2,4,64,128]{5,4,2,3,1,0:T(8,128)(2,1)}, u32[]{:S(2)}, u32[]{:S(2)}) %all-to-all-start) | async-done | bytes 4194336 | tf_op jit(solution)/shard_map/all_to_all | solution.py:17
  303.7 3.9 all-to-all-start.1
  308.2 2.6 fusion.4
  310.9 4.3 fusion.54
  315.3 58.0 %all-gather.11.cloned.1.call-done = bf16[8192,256]{1,0:T(8,128)(2,1)} async-done(((bf16[1024,256]{1,0:T(8,128)(2,1)}), bf16[8192,256]{1,0:T(8,128)(2,1)}) %all-gather.11.cloned.1.call-update) | async-done | bytes 4194320 | tf_op jit(solution)/shard_map/all_gather | solution.py:106
  373.2 3.2 convolution_convert_fusion
  376.7 5.4 copy.135
  382.1 20.3 %all-to-all-done.1 = bf16[32,2,4,64,128]{4,3,1,2,0:T(8,128)(2,1)} async-done(((bf16[32,2,4,64,128]{4,3,1,2,0:T(8,128)(2,1)}), bf16[32,2,4,64,128]{4,3,1,2,0:T(8,128)(2,1)}, u32[]{:S(2)}, u32[]{:S(2)}) %all-to-all-start.1) | async-done | bytes 4194336 | tf_op jit(solution)/shard_map/all_to_all | solution.py:131
  402.4 3.3 copy.150
  405.9 2.6 copy.154
  409.1 2.3 copy.155
  411.4 132.2 %all-gather.7.cloned.1.call-done = bf16[8192,2048]{1,0:T(8,128)(2,1)} async-done(((bf16[1024,2048]{1,0:T(8,128)(2,1)}), bf16[8192,2048]{1,0:T(8,128)(2,1)}) %all-gather.7.cloned.1.call-update) | async-done | bytes 33554448 | tf_op jit(solution)/shard_map/all_gather | solution.py:104
  543.6 13.7 %fusion.56 = f32[172,2048]{1,0:T(8,128)S(1)} fusion(bf16[8192,2048]{1,0:T(8,128)(2,1)} %all-gather.7.cloned.1.call-done, bf16[172,8192]{1,0:T(8,128)(2,1)S(1)} %copy-done.6, f32[172]{0:T(256)S(1)} %add_rsqrt_fusion), kind=kOutput, calls=%fused_computation.124 | convolution fusion | flops 5775589376 | bytes 37782192 | tf_op jit(solution)/shard_map/dot_general | solution.py:109
  559.9 10.6 %bitcast_reduce_fusion = (f32[4,2,8,43]{3,2,1,0:T(8,128)S(1)}, f32[4,2,2048,43,8]{2,3,4,1,0:T(8,128)}) fusion(pred[4,2048]{1,0:T(4,128)(4,1)S(1)} %iota_compare_fusion, bf16[2,4,2048,128,1]{3,2,4,0,1:T(8,128)(2,1)S(1)} %bitcast.195, bf16[4,43,2,8,64]{4,1,3,2,0:T(8,128)(2,1)S(1)} %bitcast.234, bf16[4,43,2,8,64]{4,1,3,2,0:T(8,128)(2,1)S(1)} %bitcast.232), kind=kOutput, calls=%fused_computation.3 | convolution fusion | flops 1461155072 | bytes 27462400 | tf_op jit(solution)/shard_map/stkgd,kscd->skgtc/dot_general | solution.py:138
  572.1 9.6 %fusion.2 = f32[4,2,8,43]{3,2,1,0:T(8,128)S(1)} fusion(f32[4,2,2048,43,8]{2,3,4,1,0:T(8,128)} %get-tuple-element.24, f32[4,2,8,43]{3,2,1,0:T(8,128)S(1)} %max.12, pred[4,2048]{1,0:T(4,128)(4,1)S(1)} %iota_compare_fusion), kind=kLoop, calls=%fused_computation.7 | loop fusion | flops 22541632 | bytes 22574592 | tf_op jit(solution)/shard_map/reduce_sum | solution.py:153
  581.6 10.9 %fusion.3 = f32[4,2,8,43,128]{4,3,2,1,0:T(8,128)S(1)} fusion(bf16[2,4,2048,128,1]{3,2,4,0,1:T(8,128)(2,1)S(1)} %bitcast.230, f32[4,2,2048,43,8]{2,3,4,1,0:T(8,128)} %get-tuple-element.24, f32[4,2,8,43]{3,2,1,0:T(8,128)S(1)} %add.84, f32[4,2,8,43]{3,2,1,0:T(8,128)S(1)} %max.12, pred[4,2048]{1,0:T(4,128)(4,1)S(1)} %iota_compare_fusion), kind=kOutput, calls=%fused_computation.8 | convolution fusion | flops 1471021056 | bytes 28177920 | tf_op jit(solution)/shard_map/skgtc,kscd->stkgd/dot_general | solution.py:158
  (111 shorter events, 37.9 us)
Async XLA Ops:
  7.2 2.8 copy-start
  7.2 301.0 %all-gather.5.cloned.1.call-start = ((), (), s32[]{:S(2)}) async-start(), calls=%async_computation.2 | async-start | bytes 3604480 | tf_op jit(solution)/shard_map/all_gather | solution.py:98
  10.0 9.6 %copy-start.7 = (s32[32,22]{0,1:T(8,128)S(1)}, s32[32,22]{0,1:T(8,128)}, u32[]{:S(2)}) copy-start(s32[32,22]{0,1:T(8,128)} %param.12) | copy-start | bytes 8452
  83.2 62.3 %copy-start.10 = (u32[32]{0:T(128)S(1)}, u32[32]{0:T(128)}, u32[]{:S(2)}) copy-start(u32[32]{0:T(128)} %constant.86) | copy-start | bytes 388
  144.1 2.6 collective-permute-start
  149.2 161.6 %all-gather.9.cloned.1.call-start = ((), (), s32[]{:S(2)}) async-start(), calls=%async_computation.4 | async-start | bytes 4718592 | tf_op jit(solution)/shard_map/all_gather | solution.py:105
  150.0 223.2 %all-gather.11.cloned.1.call-start = ((), (), s32[]{:S(2)}) async-start(), calls=%async_computation.5 | async-start | bytes 4718592 | tf_op jit(solution)/shard_map/all_gather | solution.py:106
  150.7 392.9 %all-gather.7.cloned.1.call-start = ((), (), s32[]{:S(2)}) async-start(), calls=%async_computation.3 | async-start | bytes 37748736 | tf_op jit(solution)/shard_map/all_gather | solution.py:104
  175.7 128.0 %all-to-all-start = ((bf16[32,1,2,4,64,128]{5,4,2,3,1,0:T(8,128)(2,1)}), bf16[32,1,2,4,64,128]{5,4,2,3,1,0:T(8,128)(2,1)}, u32[]{:S(2)}, u32[]{:S(2)}) async-start(bf16[32,1,2,4,64,128]{5,4,2,3,1,0:T(8,128)(2,1)} %fusion.10), calls=%async_computation | async-start | bytes 8388608 | tf_op jit(solution)/shard_map/all_to_all | solution.py:17
  303.7 3.9 copy-start.9
  303.7 3.9 copy-start.11
  303.7 98.8 %all-to-all-start.1 = ((bf16[32,2,4,64,128]{4,3,1,2,0:T(8,128)(2,1)}), bf16[32,2,4,64,128]{4,3,1,2,0:T(8,128)(2,1)}, u32[]{:S(2)}, u32[]{:S(2)}) async-start(bf16[32,2,4,64,128]{4,3,1,2,0:T(8,128)(2,1)} %bitcast.228), calls=%async_computation.1 | async-start | bytes 8388608 | tf_op jit(solution)/shard_map/all_to_all | solution.py:131
  310.8 62.4 %copy-start.6 = (bf16[172,8192]{1,0:T(8,128)(2,1)S(1)}, bf16[172,8192]{1,0:T(8,128)(2,1)}, u32[]{:S(2)}) copy-start(bf16[172,8192]{1,0:T(8,128)(2,1)} %all-gather.5.cloned.1.call-done) | copy-start | bytes 8454148
  402.4 3.4 copy-start.2
  405.8 3.3 copy-start.4
  557.7 2.2 copy-start.3
  559.9 10.6 %copy-start.8 = (pred[43,43]{0,1:T(8,128)(4,1)S(1)}, pred[43,43]{0,1:T(8,128)(4,1)}, u32[]{:S(2)}) copy-start(pred[43,43]{0,1:T(8,128)(4,1)} %constant.63.clone) | copy-start | bytes 5551
  572.1 9.6 %copy-start.5 = (bf16[1,2,4,32,64,128]{5,4,3,1,2,0:T(8,128)(2,1)S(1)}, bf16[1,2,4,32,64,128]{5,4,3,1,2,0:T(8,128)(2,1)}, u32[]{:S(2)}) copy-start(bf16[1,2,4,32,64,128]{5,4,3,1,2,0:T(8,128)(2,1)} %copy-done.4) | copy-start | bytes 12582916
  592.5 1.9 copy-start.1
Sparse Core Ops, SparseCore 0:
  149.3 96.1 all-gather.4
  247.4 54.4 all-gather.8
  303.8 69.3 all-gather.10
  375.0 168.5 all-gather.6
